TPU v7x, 256 devices: a whole 4x4x8 slice. The times are simulated.
256 devices in a mesh: expert: 64 (over z_hi, y, x), shard: 4 (over z_lo, core).
Axes of the slice: x: 4, y: 4, z: 8 (z_hi: 4, z_lo: 2; z = z_hi * 2 + z_lo), core: 2. Of those that a mesh axis runs over, the one named last changes fastest.
Arguments:
- w_gate: float32 [64, 2048, 1024], P('expert', 'shard'), may hold values from -0.1875 to 0.1875
- avg_gate: float32 [64, 2048, 1024], P('expert', 'shard'), may hold values from -0.125 to 0.125
- w_up: float32 [64, 2048, 1024], P('expert', 'shard'), may hold values from -0.1875 to 0.1875
- avg_up: float32 [64, 2048, 1024], P('expert', 'shard'), may hold values from -0.125 to 0.125
- mix_share: float32 [64], P('expert'), may hold values from 0.2 to 0.8
- router_weight: float32 [2048, 64], P('shard', 'expert'), may hold values from -0.125 to 0.125
- router_gain: float32 [2048], P('shard'), may hold values from 0.25 to 1.75
Outputs:
- serve_gate: bfloat16 [64, 2048, 1024], P('expert')
- serve_up: bfloat16 [64, 2048, 1024], P('expert')
- scale_gate: float32 [64, 1024], P('expert')
- scale_up: float32 [64, 1024], P('expert')
- serve_router: bfloat16 [2048, 64], replicated
All inputs are finite; a program needn't handle non-finite values.
Results may differ from a plain program's by a relative error of at most 0.001.
Values may be sent and summed in bfloat16 or wider, within the bound.
A program may use at most 64 MiB of HBM per device.

v0:
```python
import jax
import jax.numpy as jnp
from jax import lax
from jax.sharding import PartitionSpec as P


def copy_for_each(x, axis):
    devices = lax.axis_size(axis)
    return lax.all_to_all(jnp.broadcast_to(x[None], (devices, *x.shape)), axis, 0, 0, tiled=True)


def taken_together(x, axis):
    return copy_for_each(x, axis).sum(axis=0)


def packed_total(arrays, axis):
    ravelled, at, done = (jnp.concatenate([a.reshape(-1) for a in arrays]), 0, [])
    subtotal = taken_together(ravelled, axis)
    for a in arrays:
        done.append(subtotal[at : at + a.size].reshape(a.shape))
        at += a.size
    return tuple(done)


def in_one_piece(arrays, axis, dim, along):
    widths = [a.shape[along] for a in arrays]
    both = jnp.concatenate(arrays, axis=along)
    out = lax.all_gather(both, axis, axis=dim, tiled=True)
    return tuple(jnp.split(out, [sum(widths[:k]) for k in range(1, len(widths))], axis=along))


def joined_along(pieces, dim):
    pieces = jnp.moveaxis(pieces, 0, dim)
    shape = pieces.shape
    return pieces.reshape(*shape[:dim], shape[dim] * shape[dim + 1], *shape[dim + 2 :])


def collect(x, axis, dim):
    return joined_along(copy_for_each(x, axis), dim)


def per_device(w_gate, avg_gate, w_up, avg_up, mix_share, router_weight, router_gain):
    fresh_gate = mix_share[:, None, None] * w_gate + (1.0 - mix_share[:, None, None]) * avg_gate
    fresh_up = mix_share[:, None, None] * w_up + (1.0 - mix_share[:, None, None]) * avg_up
    total_gate, total_up = packed_total(
        (jnp.sum(fresh_gate * fresh_gate, axis=1), jnp.sum(fresh_up * fresh_up, axis=1)), "shard"
    )
    scale_gate = jnp.sqrt(total_gate)
    scale_up = jnp.sqrt(total_up)
    narrow_gate, narrow_up = (
        (fresh_gate / jnp.expand_dims(scale_gate, 1)).astype(jnp.bfloat16),
        (fresh_up / jnp.expand_dims(scale_up, 1)).astype(jnp.bfloat16),
    )
    serve_gate, serve_up = in_one_piece((narrow_gate, narrow_up), "shard", 1, 0)
    part_router = (router_weight * router_gain[:, None]).astype(jnp.bfloat16)
    row_router = collect(part_router, "shard", 0)
    serve_router = collect(row_router, "expert", 1)
    return (serve_gate, serve_up, scale_gate, scale_up, serve_router)


def solution(mesh):
    return jax.shard_map(
        per_device,
        mesh=mesh,
        in_specs=(
            P("expert", "shard", None),
            P("expert", "shard", None),
            P("expert", "shard", None),
            P("expert", "shard", None),
            P("expert"),
            P("shard", "expert"),
            P("shard"),
        ),
        out_specs=(
            P("expert", None, None),
            P("expert", None, None),
            P("expert", None),
            P("expert", None),
            P(),
        ),
        check_vma=False,
    )
```

profile of v0, /device:TPU:1, one launch (start us, length us, event | category | flops | bytes accessed | tf_op | source)
XLA Modules:
  0.0 130.6 jit_solution(11716551633294686279)
XLA Ops:
  7.2 0.0 all-gather.2.cloned.1.call-start
  7.9 0.0 copy-start
  7.9 0.0 copy-start.1
  7.9 2.8 %multiply_reduce_fusion.1 = f32[1024]{0:T(1024)S(1)} fusion(f32[1,512,1024]{2,1,0:T(8,128)} %param.8, f32[]{:T(128)} %bitcast.1, f32[1,512,1024]{2,1,0:T(8,128)} %param.7, f32[]{:T(128)} %bitcast.19), kind=kLoop, calls=%fused_computation.5 | loop fusion | flops 2620416 | bytes 4198408 | tf_op jit(solution)/shard_map/reduce_sum | solution.py:46
  10.7 0.1 copy-done
  10.7 0.6 copy-done.1
  11.3 0.5 multiply_reduce_fusion
  11.9 8.7 %all_to_all.16 = f32[4,1,2048]{2,1,0:T(1,128)S(1)} all-to-all(f32[4,1,2048]{2,1,0:T(1,128)S(1)} %broadcast_in_dim.12), channel_id=1, replica_groups=mesh['expert'=64,'shard'=4] {'shard'}, dimensions={0} | all-to-all | bytes 65536 | tf_op jit(solution)/shard_map/all_to_all | solution.py:9
  20.7 0.0 copy-start.2
  20.7 0.0 copy-start.3
  20.7 4.0 %divide_convert_fusion = (bf16[1,512,1024]{2,1,0:T(8,128)(2,1)S(1)}, bf16[1,512,1024]{2,1,0:T(8,128)(2,1)S(1)}) fusion(f32[1024]{0:T(1024)S(1)} %get-tuple-element.8, f32[1,512,1024]{2,1,0:T(8,128)S(1)} %copy-done, f32[]{:T(128)} %bitcast.1, f32[1,512,1024]{2,1,0:T(8,128)} %param.9, f32[]{:T(128)} %bitcast.21, f32[1024]{0:T(1024)S(1)} %get-tuple-element.7, ...), kind=kLoop, calls=%fused_computation.1 | loop fusion | flops 5242880 | bytes 10493960 | tf_op jit(solution)/shard_map/convert_element_type | solution.py:52
  24.6 0.0 copy-done.2
  24.7 0.0 copy-done.3
  24.7 1.5 %pad_maximum_fusion = bf16[2,512,1024]{2,1,0:T(8,128)(2,1)} fusion(bf16[1,512,1024]{2,1,0:T(8,128)(2,1)S(1)} %get-tuple-element.9, bf16[1,512,1024]{2,1,0:T(8,128)(2,1)S(1)} %get-tuple-element.10), kind=kLoop, calls=%fused_computation | loop fusion | flops 1048576 | bytes 4194304 | tf_op jit(solution)/shard_map/concatenate | solution.py:27
  26.2 0.0 copy-start.4
  26.2 0.0 copy-start.5
  26.2 0.0 all-gather.2.cloned.1.call-update
  26.2 0.7 copy-done.4
  26.8 0.0 copy-done.5
  26.9 0.5 broadcast.13
  27.4 0.7 reduce.7
  28.1 6.2 %all_to_all.17 = bf16[4,2,256]{2,1,0:T(2,128)(2,1)S(1)} all-to-all(bf16[4,2,256]{2,1,0:T(2,128)(2,1)S(1)} %reshape.54), channel_id=1, replica_groups=mesh['expert'=64,'shard'=4] {'shard'}, dimensions={0} | all-to-all | bytes 8192 | tf_op jit(solution)/shard_map/all_to_all | solution.py:9
  34.4 0.3 broadcast_bitcast_fusion
  34.6 2.2 %reduce.8 = bf16[64,2048]{1,0:T(8,128)(2,1)S(1)} reduce(bf16[64,1,2048]{2,1,0:T(2,128)(2,1)S(1)} %broadcast_bitcast_fusion, bf16[]{:T(256)} %broadcast.13), dimensions={1}, to_apply=%broadcast_bitcast_fusion.reduce_sub_computation | reduce | bytes 524290
  36.8 0.2 reshape.56
  37.0 29.5 %all_to_all.18 = bf16[64,2,1024]{2,1,0:T(2,128)(2,1)S(1)} all-to-all(bf16[64,2,1024]{2,1,0:T(2,128)(2,1)S(1)} %reshape.56), channel_id=1, replica_groups=mesh['expert'=64,'shard'=4] {'expert'}, dimensions={0} | all-to-all | bytes 524288 | tf_op jit(solution)/shard_map/all_to_all | solution.py:9
  66.5 0.2 reshape.57
  66.7 0.9 copy.21
  67.5 50.2 %all-gather.2.cloned.1.call-done = bf16[2,2048,1024]{2,1,0:T(8,128)(2,1)} async-done(((bf16[2,512,1024]{2,1,0:T(8,128)(2,1)}), bf16[2,2048,1024]{2,1,0:T(8,128)(2,1)}) %all-gather.2.cloned.1.call-update) | async-done | bytes 8388624 | tf_op jit(solution)/shard_map/all_gather | solution.py:28
  117.8 6.0 %fusion = (bf16[1,2048,1024]{2,1,0:T(8,128)(2,1)}, bf16[1,2048,1024]{2,1,0:T(8,128)(2,1)}) fusion(bf16[2,2048,1024]{2,1,0:T(8,128)(2,1)} %all-gather.2.cloned.1.call-done), kind=kLoop, calls=%fused_computation.12 | loop fusion | bytes 16777216 | tf_op jit(solution)/shard_map/split | solution.py:29
  (10 shorter events, 0.2 us)
Async XLA Ops:
  7.2 110.6 %all-gather.2.cloned.1.call-start = ((), (), s32[]{:S(2)}) async-start(), calls=%async_computation.3 | async-start | bytes 10485760 | tf_op jit(solution)/shard_map/all_gather | solution.py:28
  7.9 2.9 %copy-start = (f32[1,512,1024]{2,1,0:T(8,128)S(1)}, f32[1,512,1024]{2,1,0:T(8,128)}, u32[]{:S(2)}) copy-start(f32[1,512,1024]{2,1,0:T(8,128)} %param.10) | copy-start | bytes 6291460
  7.9 3.5 %copy-start.1 = (f32[1,512,1024]{2,1,0:T(8,128)S(1)}, f32[1,512,1024]{2,1,0:T(8,128)}, u32[]{:S(2)}) copy-start(f32[1,512,1024]{2,1,0:T(8,128)} %param.9) | copy-start | bytes 6291460
  20.7 4.0 %copy-start.2 = (f32[1024]{0:T(1024)}, f32[1024]{0:T(1024)S(1)}, u32[]{:S(2)}) copy-start(f32[1024]{0:T(1024)S(1)} %get-tuple-element.7) | copy-start | bytes 12292
  20.7 4.0 %copy-start.3 = (f32[1024]{0:T(1024)}, f32[1024]{0:T(1024)S(1)}, u32[]{:S(2)}) copy-start(f32[1024]{0:T(1024)S(1)} %get-tuple-element.8) | copy-start | bytes 12292
  26.2 0.7 copy-start.4
  26.2 0.7 copy-start.5
Sparse Core Ops, SparseCore 0:
  26.3 91.3 all-gather.1
where the time goes:
time: 131 us
  waiting for transfers between devices  50.2 us (38%)
  blocking collectives  44.4 us (34%)
  between operations  14.8 us (11%)
  other arithmetic  11.6 us (9%)
  local copies, waits for them, and re-layouts  9.54 us (7%)
    all_gather x1, waiting for transfers between devices, in_one_piece(): out = lax.all_gather(both, axis, axis=dim, tiled=True)  50.2 us
    all_to_all x3, blocking collectives, copy_for_each(): lax.all_to_all(jnp.broadcast_to(x[None], (devices, *x.shape)), axis, 0, 0...  44.4 us
    split x1, local copies, waits for them, and re-layouts, in_one_piece(): jnp.split(out, [sum(widths[:k]) for k in range(1, len(widths))], axis=along)  6.02 us
    convert_element_type x1, other arithmetic, per_device(): (fresh_up / jnp.expand_dims(scale_up, 1)).astype(jnp.bfloat16)  3.95 us
    unnamed x2, other arithmetic  2.83 us
    reduce_sum x1, other arithmetic, per_device(): jnp.sum(fresh_gate * fresh_gate, axis=1)  2.78 us
  transfers between devices with their start and end apart: 1, of which 1 were waited for; matrix products, arithmetic and copies ran while one was open for 4% of the time, Pallas kernels for 0%

commit v1 on v0

v1 whole, which is shorter than its diff:
```python
import jax
import jax.numpy as jnp
from jax import lax
from jax.experimental import pallas as pl
from jax.experimental.pallas import tpu as pltpu
from jax.sharding import PartitionSpec as P

MESH = pl.DeviceIdType.MESH
LANES = 128
BLOCK = 64


def mix_and_send(
    w_gate, avg_gate, w_up, avg_up, share, router_weight, router_gain,
    out_gate, out_up, out_scale_gate, out_scale_up, out_router,
    fresh, other, sums, router,
    load_sem, sum_send, sum_recv, across_send, across_recv, beside_send, beside_recv, passed_send, passed_recv,
    router_send, router_recv,
):
    rows, columns = fresh.shape[1], fresh.shape[2]
    per_matrix = columns // LANES
    chunks = 2 * per_matrix
    expert, shard = lax.axis_index("expert"), lax.axis_index("shard")
    far, core = shard // 2, shard % 2
    hi, y, x = expert // 16, (expert // 4) % 4, expert % 4
    across, beside = (shard + 2) % 4, far * 2 + (1 - core)
    peers = [(shard + d) % 4 for d in (1, 2, 3)]
    up_hi, down_hi = (expert + 16) % 64, (expert + 48) % 64
    along_x = [hi * 16 + y * 4 + (x + d) % 4 for d in (1, 2, 3)]
    along_y = [hi * 16 + ((y + d) % 4) * 4 + x for d in (1, 2, 3)]

    def place(k):
        return k // per_matrix, pl.ds((k % per_matrix) * LANES, LANES)

    def load(k, which):
        m, cols = place(k)
        source = ((w_gate, avg_gate), (w_up, avg_up))[m][which]
        target = (fresh, other)[which]
        return pltpu.make_async_copy(source.at[0, :, cols], target.at[m, :, cols], load_sem.at[k, which])

    for k in range(chunks):
        load(k, 0).start()
        load(k, 1).start()

    barrier = pltpu.get_barrier_semaphore()
    greeted = [(expert, p) for p in peers] + [(e, shard) for e in (up_hi, down_hi, *along_x, *along_y)]
    for device in greeted:
        pl.semaphore_signal(barrier, inc=1, device_id=device, device_id_type=MESH)

    keep = share[0]
    rest = 1.0 - keep
    own = pl.multiple_of(shard * rows, rows)

    def mix(k):
        m, cols = place(k)
        load(k, 0).wait()
        load(k, 1).wait()

        def block(i, total):
            at = pl.ds(pl.multiple_of(i * BLOCK, BLOCK), BLOCK)
            value = keep * fresh[m, at, cols] + rest * other[m, at, cols]
            fresh[m, at, cols] = value
            return total + jnp.sum((value * value).reshape(BLOCK // 8, 8, LANES), axis=0)

        total = lax.fori_loop(0, rows // BLOCK, block, jnp.zeros((8, LANES), jnp.float32))
        sums[k, shard] = jnp.sum(total, axis=0, keepdims=True)

    def sum_copy(k, d):
        return pltpu.make_async_remote_copy(
            sums.at[k, shard], sums.at[k, shard], sum_send.at[k, d], sum_recv.at[k, d],
            device_id=(expert, peers[d]), device_id_type=MESH,
        )

    def out_of(k):
        return (out_gate, out_up)[k // per_matrix]

    def across_copy(k):
        piece = out_of(k).at[pl.ds(own, rows), place(k)[1]]
        return pltpu.make_async_remote_copy(
            piece, piece, across_send.at[k], across_recv.at[k], device_id=(expert, across), device_id_type=MESH
        )

    def beside_copy(k):
        piece = out_of(k).at[pl.ds(own, rows), place(k)[1]]
        return pltpu.make_async_remote_copy(
            piece, piece, beside_send.at[k], beside_recv.at[k], device_id=(expert, beside), device_id_type=MESH
        )

    def passed_copy(k):
        piece = out_of(k).at[pl.ds(pl.multiple_of(across * rows, rows), rows), place(k)[1]]
        return pltpu.make_async_remote_copy(
            piece, piece, passed_send.at[k], passed_recv.at[k], device_id=(expert, beside), device_id_type=MESH
        )

    def scale_and_send(k):
        m, cols = place(k)
        for d in range(3):
            sum_copy(k, d).wait_recv()
        scale = jnp.sqrt(sums[k, 0] + sums[k, 1] + sums[k, 2] + sums[k, 3])
        (out_scale_gate, out_scale_up)[m][:, cols] = scale
        inverse = 1.0 / scale
        target = out_of(k)

        def block(i, carry):
            at = pl.multiple_of(i * BLOCK, BLOCK)
            value = fresh[m, pl.ds(at, BLOCK), cols] * inverse
            target[pl.ds(pl.multiple_of(own + at, BLOCK), BLOCK), cols] = value.astype(jnp.bfloat16)
            return carry

        lax.fori_loop(0, rows // BLOCK, block, 0)
        across_copy(k).start()
        beside_copy(k).start()

    def router_copy(piece, n, device):
        return pltpu.make_async_remote_copy(
            piece, piece, router_send.at[n], router_recv.at[n], device_id=device, device_id_type=MESH
        )

    tile = pl.multiple_of((expert % 16) * 8, 8)
    part = router.at[core, hi, pl.ds(pl.multiple_of(tile + far * 4, 4), 4)]
    stage_far = [router_copy(part, 0, (expert, across))]
    mine = router.at[core, hi, pl.ds(tile, 8)]
    stage_hi = [router_copy(mine, 1, (up_hi, shard)), router_copy(mine, 2, (down_hi, shard))]
    stage_hi_on = [router_copy(router.at[core, (hi + 3) % 4, pl.ds(tile, 8)], 3, (up_hi, shard))]
    line = router.at[core, :, pl.ds(tile, 8)]
    stage_x = [router_copy(line, 4 + d, (along_x[d], shard)) for d in range(3)]
    plane = router.at[core, :, pl.ds(pl.multiple_of(y * 32, 32), 32)]
    stage_y = [router_copy(plane, 7 + d, (along_y[d], shard)) for d in range(3)]
    stage_core = [router_copy(router.at[core], 10, (expert, beside))]
    stages = [stage_far, stage_hi, stage_hi_on, stage_x, stage_y, stage_core]

    def router_stage(n):
        if n > 0:
            for c in stages[n - 1]:
                c.wait_recv()
        if n < len(stages):
            for c in stages[n]:
                c.start()

    mix(0)
    product = (router_weight[...] * router_gain[...]).astype(jnp.bfloat16).astype(jnp.float32)
    for j in range(4):
        router[core, hi, pl.ds(tile + far * 4 + j, 1)] = product[:, j * LANES : (j + 1) * LANES]

    pl.semaphore_wait(barrier, len(greeted))
    ahead = 2
    for k in range(ahead):
        if k:
            mix(k)
        for d in range(3):
            sum_copy(k, d).start()
    for k in range(chunks):
        scale_and_send(k)
        if k == 0:
            router_stage(0)
        if k + ahead < chunks:
            mix(k + ahead)
            for d in range(3):
                sum_copy(k + ahead, d).start()
    for k in range(chunks):
        across_copy(k).wait_recv()
        passed_copy(k).start()
        if k >= 4 and k - 3 <= len(stages):
            router_stage(k - 3)
        if k - 3 == len(stages):
            for c in (0, 1):
                for f in (0, 1):
                    for j in range(4):
                        at = (f * 2 + c) * 4 * LANES + j * LANES
                        for h in range(4):
                            piece = router[c, h, pl.ds(f * 4 + j, 16, stride=8), :]
                            out_router[h * 16 : (h + 1) * 16, at : at + LANES] = piece.astype(jnp.bfloat16)
    for k in range(chunks):
        for d in range(3):
            sum_copy(k, d).wait_send()
        across_copy(k).wait_send()
        beside_copy(k).wait_send()
        beside_copy(k).wait_recv()
    for stage in stages:
        for c in stage:
            c.wait_send()
    for k in range(chunks):
        passed_copy(k).wait_send()
        passed_copy(k).wait_recv()


def per_device(w_gate, avg_gate, w_up, avg_up, mix_share, router_weight, router_gain):
    _, rows, columns = w_gate.shape
    chunks = 2 * columns // LANES
    outs = pl.pallas_call(
        mix_and_send,
        out_shape=(
            pltpu.VMEM((4 * rows, columns), jnp.bfloat16),
            pltpu.VMEM((4 * rows, columns), jnp.bfloat16),
            pltpu.VMEM((1, columns), jnp.float32),
            pltpu.VMEM((1, columns), jnp.float32),
            pltpu.VMEM((64, 4 * rows), jnp.bfloat16),
        ),
        in_specs=[pl.BlockSpec(memory_space=pl.ANY)] * 4
        + [pl.BlockSpec(memory_space=pltpu.SMEM)]
        + [pl.BlockSpec(memory_space=pltpu.VMEM)] * 2,
        out_specs=[pl.BlockSpec(memory_space=pltpu.VMEM)] * 5,
        scratch_shapes=[
            pltpu.VMEM((2, rows, columns), jnp.float32),
            pltpu.VMEM((2, rows, columns), jnp.float32),
            pltpu.VMEM((chunks, 4, 1, LANES), jnp.float32),
            pltpu.VMEM((2, 4, 128, LANES), jnp.float32),
            pltpu.SemaphoreType.DMA((chunks, 2)),
            pltpu.SemaphoreType.DMA((chunks, 3)),
            pltpu.SemaphoreType.DMA((chunks, 3)),
        ]
        + [pltpu.SemaphoreType.DMA((chunks,))] * 6
        + [pltpu.SemaphoreType.DMA((11,))] * 2,
        compiler_params=pltpu.CompilerParams(
            collective_id=0, has_side_effects=True, vmem_limit_bytes=24 * 1024 * 1024
        ),
    )(
        w_gate, avg_gate, w_up, avg_up, mix_share,
        router_weight.reshape(1, rows), router_gain.reshape(1, rows),
    )
    gate, up, scale_gate, scale_up, router = outs
    return gate[None], up[None], scale_gate, scale_up, router.T


def solution(mesh):
    return jax.shard_map(
        per_device,
        mesh=mesh,
        in_specs=(
            P("expert", "shard", None),
            P("expert", "shard", None),
            P("expert", "shard", None),
            P("expert", "shard", None),
            P("expert"),
            P("shard", "expert"),
            P("shard"),
        ),
        out_specs=(
            P("expert", None, None),
            P("expert", None, None),
            P("expert", None),
            P("expert", None),
            P(),
        ),
        check_vma=False,
    )
```

time: 131 us -> 94.7 us (0.72)
  Pallas kernels: 0 us -> 79.5 us
  waiting for transfers between devices: 50.2 us -> 0 us
  blocking collectives: 44.4 us -> 0 us
  between operations: 14.8 us -> 1.3 us
  other arithmetic: 11.6 us -> 0 us
  local copies, waits for them, and re-layouts: 9.54 us -> 13.6 us
    pallas_call x0 -> x1, Pallas kernels: none -> 79.5 us  [per_device(): pl.pallas_call(mix_and_send, out_shape=(pltpu.VMEM((4 * rows, columns), j...]
    all_gather x1 -> x0, waiting for transfers between devices: 50.2 us -> none  [in_one_piece(): out = lax.all_gather(both, axis, axis=dim, tiled=True)]
    all_to_all x3 -> x0, blocking collectives: 44.4 us -> none  [copy_for_each(): lax.all_to_all(jnp.broadcast_to(x[None], (devices, *x.shape)), axis, 0, 0...]
    unnamed x20 -> x17, local copies, waits for them, and re-layouts: 2.6 us -> 13.6 us
    split x1 -> x0, local copies, waits for them, and re-layouts: 6.02 us -> none  [in_one_piece(): jnp.split(out, [sum(widths[:k]) for k in range(1, len(widths))], axis=along)]
    convert_element_type x2 -> x0, other arithmetic: 3.97 us -> none  [the longest x1 3.95 us: per_device(): (fresh_up / jnp.expand_dims(scale_up, 1)).astype(jnp.bfloat16)]
    reduce_sum x3 -> x0, other arithmetic: 3.32 us -> none  [the longest x1 2.78 us: per_device(): jnp.sum(fresh_gate * fresh_gate, axis=1)]
    unnamed x2 -> x0, other arithmetic: 2.83 us -> none
  transfers between devices with their start and end apart: 1 -> 0, of which waited for: 1 -> 0; matrix products, arithmetic and copies ran while one was open for 4% -> 0% of each run, Pallas kernels for 0% -> 0%
where the time goes in v1:
time: 94.7 us; the launch traced here: 94.5 us
  Pallas kernels  79.5 us (84%)
  local copies, waits for them, and re-layouts  13.6 us (14%)
  between operations  1.3 us (1%)
    pallas_call x1, Pallas kernels, per_device(): pl.pallas_call(mix_and_send, out_shape=(pltpu.VMEM((4 * rows, columns), j...  79.5 us
    unnamed x17, local copies, waits for them, and re-layouts  13.6 us

profile of v1, /device:TPU:1, one launch (start us, length us, event | category | flops | bytes accessed | tf_op | source)
XLA Modules:
  0.0 94.5 jit_solution(97235154659962219)
XLA Ops:
  1.3 0.0 copy-start
  1.3 1.6 %copy-done = f32[1,512,1024]{2,1,0:T(8,128)S(1)} copy-done((f32[1,512,1024]{2,1,0:T(8,128)S(1)}, f32[1,512,1024]{2,1,0:T(8,128)}, u32[]{:S(2)}) %copy-start) | copy-done | bytes 2097176
  2.9 0.0 copy-start.1
  2.9 1.6 %copy-done.1 = f32[1,512,1024]{2,1,0:T(8,128)S(1)} copy-done((f32[1,512,1024]{2,1,0:T(8,128)S(1)}, f32[1,512,1024]{2,1,0:T(8,128)}, u32[]{:S(2)}) %copy-start.1) | copy-done | bytes 2097176
  4.5 0.0 copy-start.2
  4.5 1.6 %copy-done.2 = f32[1,512,1024]{2,1,0:T(8,128)S(1)} copy-done((f32[1,512,1024]{2,1,0:T(8,128)S(1)}, f32[1,512,1024]{2,1,0:T(8,128)}, u32[]{:S(2)}) %copy-start.2) | copy-done | bytes 2097176
  6.1 0.0 copy-start.3
  6.1 1.6 %copy-done.3 = f32[1,512,1024]{2,1,0:T(8,128)S(1)} copy-done((f32[1,512,1024]{2,1,0:T(8,128)S(1)}, f32[1,512,1024]{2,1,0:T(8,128)}, u32[]{:S(2)}) %copy-start.3) | copy-done | bytes 2097176
  7.6 0.0 copy-start.4
  7.6 0.7 copy-done.4
  8.3 0.0 copy-start.5
  8.3 0.7 copy-done.5
  9.0 79.5 %shard_map.110 = (bf16[2048,1024]{1,0:T(8,128)(2,1)S(1)}, bf16[2048,1024]{1,0:T(8,128)(2,1)S(1)}, f32[1,1024]{1,0:T(1,128)S(1)}, f32[1,1024]{1,0:T(1,128)S(1)}, bf16[64,2048]{1,0:T(8,128)(2,1)S(1)}) custom-call(f32[1,512,1024]{2,1,0:T(8,128)S(1)} %copy-done, f32[1,512,1024]{2,1,0:T(8,128)S(1)} %copy-done.1, f32[1,512,1024]{2,1,0:T(8,128)S(1)} %copy-done.2, ...), custom_call_target="tpu_custom_call" | custom-call | tf_op jit(solution)/shard_map/pallas_call | solution.py:190
  88.6 2.0 %copy.17 = bf16[1,2048,1024]{2,1,0:T(8,128)(2,1)} copy(bf16[1,2048,1024]{2,1,0:T(8,128)(2,1)S(1)} %bitcast.6) | data formatting | bytes 8388608
  90.6 2.0 %copy.18 = bf16[1,2048,1024]{2,1,0:T(8,128)(2,1)} copy(bf16[1,2048,1024]{2,1,0:T(8,128)(2,1)S(1)} %bitcast.5) | data formatting | bytes 8388608
  92.6 0.6 copy.19
  93.2 0.6 copy.20
  93.8 0.7 copy.21
Async XLA Ops:
  1.3 1.6 %copy-start = (f32[1,512,1024]{2,1,0:T(8,128)S(1)}, f32[1,512,1024]{2,1,0:T(8,128)}, u32[]{:S(2)}) copy-start(f32[1,512,1024]{2,1,0:T(8,128)} %w_gate.1) | copy-start | bytes 6291460
  2.9 1.6 %copy-start.1 = (f32[1,512,1024]{2,1,0:T(8,128)S(1)}, f32[1,512,1024]{2,1,0:T(8,128)}, u32[]{:S(2)}) copy-start(f32[1,512,1024]{2,1,0:T(8,128)} %avg_gate.1) | copy-start | bytes 6291460
  4.5 1.6 %copy-start.2 = (f32[1,512,1024]{2,1,0:T(8,128)S(1)}, f32[1,512,1024]{2,1,0:T(8,128)}, u32[]{:S(2)}) copy-start(f32[1,512,1024]{2,1,0:T(8,128)} %w_up.1) | copy-start | bytes 6291460
  6.1 1.6 %copy-start.3 = (f32[1,512,1024]{2,1,0:T(8,128)S(1)}, f32[1,512,1024]{2,1,0:T(8,128)}, u32[]{:S(2)}) copy-start(f32[1,512,1024]{2,1,0:T(8,128)} %avg_up.1) | copy-start | bytes 6291460
  7.6 0.7 copy-start.4
  8.3 0.7 copy-start.5

commit v2 on v1

--- a/solution.py
+++ b/solution.py
@@ -11,10 +11,10 @@
 
 
 def mix_and_send(
-    w_gate, avg_gate, w_up, avg_up, share, router_weight, router_gain,
+    w_gate, avg_gate, w_up, avg_up, mix_share, router_weight, router_gain,
     out_gate, out_up, out_scale_gate, out_scale_up, out_router,
-    fresh, other, sums, router,
-    load_sem, sum_send, sum_recv, across_send, across_recv, beside_send, beside_recv, passed_send, passed_recv,
+    fresh, other, sums, router, share, factors,
+    small_sem, load_sem, sum_send, sum_recv, across_send, across_recv, beside_send, beside_recv, passed_send, passed_recv,
     router_send, router_recv,
 ):
     rows, columns = fresh.shape[1], fresh.shape[2]
@@ -38,15 +38,25 @@
         target = (fresh, other)[which]
         return pltpu.make_async_copy(source.at[0, :, cols], target.at[m, :, cols], load_sem.at[k, which])
 
-    for k in range(chunks):
-        load(k, 0).start()
-        load(k, 1).start()
-
     barrier = pltpu.get_barrier_semaphore()
     greeted = [(expert, p) for p in peers] + [(e, shard) for e in (up_hi, down_hi, *along_x, *along_y)]
     for device in greeted:
         pl.semaphore_signal(barrier, inc=1, device_id=device, device_id_type=MESH)
 
+    small = [
+        pltpu.make_async_copy(mix_share, share, small_sem.at[0]),
+        pltpu.make_async_copy(router_weight, factors.at[0], small_sem.at[1]),
+        pltpu.make_async_copy(router_gain, factors.at[1], small_sem.at[2]),
+    ]
+    small[0].start()
+    for k in range(chunks):
+        load(k, 0).start()
+        load(k, 1).start()
+        if k == 0:
+            small[1].start()
+            small[2].start()
+
+    small[0].wait()
     keep = share[0]
     rest = 1.0 - keep
     own = pl.multiple_of(shard * rows, rows)
@@ -63,13 +73,27 @@
             return total + jnp.sum((value * value).reshape(BLOCK // 8, 8, LANES), axis=0)
 
         total = lax.fori_loop(0, rows // BLOCK, block, jnp.zeros((8, LANES), jnp.float32))
-        sums[k, shard] = jnp.sum(total, axis=0, keepdims=True)
-
-    def sum_copy(k, d):
-        return pltpu.make_async_remote_copy(
-            sums.at[k, shard], sums.at[k, shard], sum_send.at[k, d], sum_recv.at[k, d],
-            device_id=(expert, peers[d]), device_id_type=MESH,
-        )
+        sums[shard, :, pl.ds(k * LANES, LANES)] = jnp.sum(total, axis=0, keepdims=True)
+
+    groups = [(0, 1), (1, 3), (3, 8), (8, chunks)]
+
+    def sum_copies(g):
+        first, last = groups[g]
+        part = sums.at[shard, :, pl.ds(first * LANES, (last - first) * LANES)]
+        return [
+            pltpu.make_async_remote_copy(
+                part, part, sum_send.at[g, d], sum_recv.at[g, d], device_id=(expert, peers[d]), device_id_type=MESH
+            )
+            for d in range(3)
+        ]
+
+    def mix_group(g):
+        for k in range(*groups[g]):
+            mix(k)
+
+    def send_sums(g):
+        for copy in sum_copies(g):
+            copy.start()
 
     def out_of(k):
         return (out_gate, out_up)[k // per_matrix]
@@ -94,9 +118,12 @@
 
     def scale_and_send(k):
         m, cols = place(k)
-        for d in range(3):
-            sum_copy(k, d).wait_recv()
-        scale = jnp.sqrt(sums[k, 0] + sums[k, 1] + sums[k, 2] + sums[k, 3])
+        for g, (first, _) in enumerate(groups):
+            if first == k:
+                for copy in sum_copies(g):
+                    copy.wait_recv()
+        at = pl.ds(k * LANES, LANES)
+        scale = jnp.sqrt(sums[0, :, at] + sums[1, :, at] + sums[2, :, at] + sums[3, :, at])
         (out_scale_gate, out_scale_up)[m][:, cols] = scale
         inverse = 1.0 / scale
         target = out_of(k)
@@ -137,51 +164,73 @@
             for c in stages[n]:
                 c.start()
 
-    mix(0)
-    product = (router_weight[...] * router_gain[...]).astype(jnp.bfloat16).astype(jnp.float32)
+    def put_router():
+        for c in (0, 1):
+            for f in (0, 1):
+                for j in range(4):
+                    at = (f * 2 + c) * 4 * LANES + j * LANES
+                    for h in range(4):
+                        piece = router[c, h, pl.ds(f * 4 + j, 16, stride=8), :]
+                        out_router[h * 16 : (h + 1) * 16, at : at + LANES] = piece.astype(jnp.bfloat16)
+
+    mix_group(0)
+    pl.semaphore_wait(barrier, len(greeted))
+    send_sums(0)
+    small[1].wait()
+    small[2].wait()
+    product = (factors[0] * factors[1]).astype(jnp.bfloat16).astype(jnp.float32)
     for j in range(4):
         router[core, hi, pl.ds(tile + far * 4 + j, 1)] = product[:, j * LANES : (j + 1) * LANES]
-
-    pl.semaphore_wait(barrier, len(greeted))
-    ahead = 2
-    for k in range(ahead):
-        if k:
-            mix(k)
-        for d in range(3):
-            sum_copy(k, d).start()
-    for k in range(chunks):
-        scale_and_send(k)
-        if k == 0:
-            router_stage(0)
-        if k + ahead < chunks:
-            mix(k + ahead)
-            for d in range(3):
-                sum_copy(k + ahead, d).start()
-    for k in range(chunks):
+    mix_group(1)
+    send_sums(1)
+    router_stage(0)
+    scale_and_send(0)
+    mix_group(2)
+    send_sums(2)
+    scale_and_send(1)
+    router_stage(1)
+    mix_group(3)
+    scale_and_send(2)
+    send_sums(3)
+    router_at = {4: 2, 7: 3, 9: 4, 11: 5, 13: 6}
+
+    def pass_on(k):
         across_copy(k).wait_recv()
         passed_copy(k).start()
-        if k >= 4 and k - 3 <= len(stages):
-            router_stage(k - 3)
-        if k - 3 == len(stages):
-            for c in (0, 1):
-                for f in (0, 1):
-                    for j in range(4):
-                        at = (f * 2 + c) * 4 * LANES + j * LANES
-                        for h in range(4):
-                            piece = router[c, h, pl.ds(f * 4 + j, 16, stride=8), :]
-                            out_router[h * 16 : (h + 1) * 16, at : at + LANES] = piece.astype(jnp.bfloat16)
+
+    for k in range(3, chunks):
+        across_copy(k - 2).wait_send()
+        scale_and_send(k)
+        pass_on(k - 3)
+        if k in router_at:
+            router_stage(router_at[k])
+    put_router()
+    for g in range(len(groups)):
+        for copy in sum_copies(g):
+            copy.wait_send()
+    for stage in stages:
+        for copy in stage:
+            copy.wait_send()
+    across_copy(0).wait_send()
+    for k in range(chunks - 3, chunks):
+        pass_on(k)
+    for k in range(chunks - 2, chunks):
+        across_copy(k).wait_send()
     for k in range(chunks):
-        for d in range(3):
-            sum_copy(k, d).wait_send()
-        across_copy(k).wait_send()
         beside_copy(k).wait_send()
         beside_copy(k).wait_recv()
-    for stage in stages:
-        for c in stage:
-            c.wait_send()
     for k in range(chunks):
         passed_copy(k).wait_send()
         passed_copy(k).wait_recv()
+
+
+def put_out(*refs):
+    sems = refs[10]
+    copies = [pltpu.make_async_copy(refs[n], refs[n + 5], sems.at[n]) for n in range(5)]
+    for copy in copies:
+        copy.start()
+    for copy in copies:
+        copy.wait()
 
 
 def per_device(w_gate, avg_gate, w_up, avg_up, mix_share, router_weight, router_gain):
@@ -196,29 +245,37 @@
             pltpu.VMEM((1, columns), jnp.float32),
             pltpu.VMEM((64, 4 * rows), jnp.bfloat16),
         ),
-        in_specs=[pl.BlockSpec(memory_space=pl.ANY)] * 4
-        + [pl.BlockSpec(memory_space=pltpu.SMEM)]
-        + [pl.BlockSpec(memory_space=pltpu.VMEM)] * 2,
+        in_specs=[pl.BlockSpec(memory_space=pl.ANY)] * 7,
         out_specs=[pl.BlockSpec(memory_space=pltpu.VMEM)] * 5,
         scratch_shapes=[
             pltpu.VMEM((2, rows, columns), jnp.float32),
             pltpu.VMEM((2, rows, columns), jnp.float32),
-            pltpu.VMEM((chunks, 4, 1, LANES), jnp.float32),
+            pltpu.VMEM((4, 1, chunks * LANES), jnp.float32),
             pltpu.VMEM((2, 4, 128, LANES), jnp.float32),
+            pltpu.SMEM((1,), jnp.float32),
+            pltpu.VMEM((2, 1, rows), jnp.float32),
+            pltpu.SemaphoreType.DMA((3,)),
             pltpu.SemaphoreType.DMA((chunks, 2)),
-            pltpu.SemaphoreType.DMA((chunks, 3)),
-            pltpu.SemaphoreType.DMA((chunks, 3)),
+            pltpu.SemaphoreType.DMA((4, 3)),
+            pltpu.SemaphoreType.DMA((4, 3)),
         ]
         + [pltpu.SemaphoreType.DMA((chunks,))] * 6
         + [pltpu.SemaphoreType.DMA((11,))] * 2,
         compiler_params=pltpu.CompilerParams(
-            collective_id=0, has_side_effects=True, vmem_limit_bytes=24 * 1024 * 1024
+            collective_id=0, has_side_effects=True, vmem_limit_bytes=55 * 1024 * 1024
         ),
     )(
         w_gate, avg_gate, w_up, avg_up, mix_share,
         router_weight.reshape(1, rows), router_gain.reshape(1, rows),
     )
-    gate, up, scale_gate, scale_up, router = outs
+    gate, up, scale_gate, scale_up, router = pl.pallas_call(
+        put_out,
+        out_shape=[jax.ShapeDtypeStruct(o.shape, o.dtype) for o in outs],
+        in_specs=[pl.BlockSpec(memory_space=pltpu.VMEM)] * 5,
+        out_specs=[pl.BlockSpec(memory_space=pl.ANY)] * 5,
+        scratch_shapes=[pltpu.SemaphoreType.DMA((5,))],
+        compiler_params=pltpu.CompilerParams(vmem_limit_bytes=1024 * 1024),
+    )(*outs)
     return gate[None], up[None], scale_gate, scale_up, router.T
 
 

time: 94.7 us -> 65 us (0.69)
  Pallas kernels: 79.5 us -> 63.6 us
  local copies, waits for them, and re-layouts: 13.6 us -> 0 us
    pallas_call x1, Pallas kernels: 79.5 us -> 60.2 us  [per_device(): pl.pallas_call(mix_and_send, out_shape=(pltpu.VMEM((4 * rows, columns), j...]
    unnamed x17 -> x0, local copies, waits for them, and re-layouts: 13.6 us -> none
    pallas_call x0 -> x1, Pallas kernels: none -> 3.45 us  [per_device(): pl.pallas_call(put_out, out_shape=[jax.ShapeDtypeStruct(o.shape, o.dtype)...]
where the time goes in v2:
time: 65 us; the launch traced here: 64.9 us
  Pallas kernels  63.6 us (98%)
  between operations  1.29 us (2%)
    pallas_call x1, Pallas kernels, per_device(): pl.pallas_call(mix_and_send, out_shape=(pltpu.VMEM((4 * rows, columns), j...  60.2 us
    pallas_call x1, Pallas kernels, per_device(): pl.pallas_call(put_out, out_shape=[jax.ShapeDtypeStruct(o.shape, o.dtype)...  3.45 us

profile of v2, /device:TPU:1, one launch (start us, length us, event | category | flops | bytes accessed | tf_op | source)
XLA Modules:
  0.0 64.9 jit_solution(3772970929742905893)
XLA Ops:
  1.3 60.2 %shard_map.110 = (bf16[2048,1024]{1,0:T(8,128)(2,1)S(1)}, bf16[2048,1024]{1,0:T(8,128)(2,1)S(1)}, f32[1,1024]{1,0:T(1,128)S(1)}, f32[1,1024]{1,0:T(1,128)S(1)}, bf16[64,2048]{1,0:T(8,128)(2,1)S(1)}) custom-call(f32[1,512,1024]{2,1,0:T(8,128)} %w_gate.1, f32[1,512,1024]{2,1,0:T(8,128)} %avg_gate.1, f32[1,512,1024]{2,1,0:T(8,128)} %w_up.1, ...), custom_call_target="tpu_custom_call" | custom-call | tf_op jit(solution)/shard_map/pallas_call | solution.py:239
  61.5 3.4 %shard_map.111 = (bf16[2048,1024]{1,0:T(8,128)(2,1)}, bf16[2048,1024]{1,0:T(8,128)(2,1)}, f32[1,1024]{1,0:T(1,128)}, f32[1,1024]{1,0:T(1,128)}, bf16[64,2048]{1,0:T(8,128)(2,1)}) custom-call(bf16[2048,1024]{1,0:T(8,128)(2,1)S(1)} %get-tuple-element.15.refs_0_, bf16[2048,1024]{1,0:T(8,128)(2,1)S(1)} %get-tuple-element.16.refs_1_, ...), custom_call_target="tpu_custom_call" | custom-call | tf_op jit(solution)/shard_map/pallas_call | solution.py:271

commit v3 on v2

--- a/solution.py
+++ b/solution.py
@@ -15,7 +15,7 @@
     out_gate, out_up, out_scale_gate, out_scale_up, out_router,
     fresh, other, sums, router, share, factors,
     small_sem, load_sem, sum_send, sum_recv, across_send, across_recv, beside_send, beside_recv, passed_send, passed_recv,
-    router_send, router_recv,
+    router_send, router_recv, entered,
 ):
     rows, columns = fresh.shape[1], fresh.shape[2]
     per_matrix = columns // LANES
@@ -38,24 +38,28 @@
         target = (fresh, other)[which]
         return pltpu.make_async_copy(source.at[0, :, cols], target.at[m, :, cols], load_sem.at[k, which])
 
-    barrier = pltpu.get_barrier_semaphore()
-    greeted = [(expert, p) for p in peers] + [(e, shard) for e in (up_hi, down_hi, *along_x, *along_y)]
-    for device in greeted:
-        pl.semaphore_signal(barrier, inc=1, device_id=device, device_id_type=MESH)
-
     small = [
         pltpu.make_async_copy(mix_share, share, small_sem.at[0]),
         pltpu.make_async_copy(router_weight, factors.at[0], small_sem.at[1]),
         pltpu.make_async_copy(router_gain, factors.at[1], small_sem.at[2]),
     ]
     small[0].start()
-    for k in range(chunks):
-        load(k, 0).start()
-        load(k, 1).start()
-        if k == 0:
-            small[1].start()
-            small[2].start()
-
+    barrier = pltpu.get_barrier_semaphore()
+    for p in peers:
+        pl.semaphore_signal(barrier, inc=1, device_id=(expert, p), device_id_type=MESH)
+    router_peers = [(up_hi, up_hi > expert), (down_hi, down_hi > expert)]
+    router_peers += [(e, e > expert) for e in along_x + along_y]
+    later = sum(after.astype(jnp.int32) for _, after in router_peers)
+    for e, after in router_peers:
+
+        @pl.when(after)
+        def _():
+            pl.semaphore_signal(barrier, inc=1, device_id=(e, shard), device_id_type=MESH)
+
+
+    for n in range(chunks):
+        load(n, 0).start()
+        load(n, 1).start()
     small[0].wait()
     keep = share[0]
     rest = 1.0 - keep
@@ -65,6 +69,9 @@
         m, cols = place(k)
         load(k, 0).wait()
         load(k, 1).wait()
+        if k == 0:
+            for copy in small[1:]:
+                copy.start()
 
         def block(i, total):
             at = pl.ds(pl.multiple_of(i * BLOCK, BLOCK), BLOCK)
@@ -174,8 +181,14 @@
                         out_router[h * 16 : (h + 1) * 16, at : at + LANES] = piece.astype(jnp.bfloat16)
 
     mix_group(0)
-    pl.semaphore_wait(barrier, len(greeted))
+    pl.semaphore_wait(barrier, len(peers) + len(router_peers) - later)
     send_sums(0)
+    for e, after in router_peers:
+
+        @pl.when(jnp.logical_not(after))
+        def _():
+            pl.semaphore_signal(entered, inc=1, device_id=(e, shard), device_id_type=MESH)
+
     small[1].wait()
     small[2].wait()
     product = (factors[0] * factors[1]).astype(jnp.bfloat16).astype(jnp.float32)
@@ -188,6 +201,11 @@
     mix_group(2)
     send_sums(2)
     scale_and_send(1)
+
+    @pl.when(later > 0)
+    def _():
+        pl.semaphore_wait(entered, later)
+
     router_stage(1)
     mix_group(3)
     scale_and_send(2)
@@ -260,7 +278,8 @@
             pltpu.SemaphoreType.DMA((4, 3)),
         ]
         + [pltpu.SemaphoreType.DMA((chunks,))] * 6
-        + [pltpu.SemaphoreType.DMA((11,))] * 2,
+        + [pltpu.SemaphoreType.DMA((11,))] * 2
+        + [pltpu.SemaphoreType.REGULAR],
         compiler_params=pltpu.CompilerParams(
             collective_id=0, has_side_effects=True, vmem_limit_bytes=55 * 1024 * 1024
         ),

time: 65 us -> 61.7 us (0.949)
  Pallas kernels: 63.6 us -> 60.3 us
    pallas_call x1, Pallas kernels: 60.2 us -> 56.8 us  [per_device(): pl.pallas_call(mix_and_send, out_shape=(pltpu.VMEM((4 * rows, columns), j...]
where the time goes in v3:
time: 61.7 us; the launch traced here: 61.6 us
  Pallas kernels  60.3 us (98%)
  between operations  1.29 us (2%)
    pallas_call x1, Pallas kernels, per_device(): pl.pallas_call(mix_and_send, out_shape=(pltpu.VMEM((4 * rows, columns), j...  56.8 us
    pallas_call x1, Pallas kernels, per_device(): pl.pallas_call(put_out, out_shape=[jax.ShapeDtypeStruct(o.shape, o.dtype)...  3.45 us

profile of v3, /device:TPU:1, one launch (start us, length us, event | category | flops | bytes accessed | tf_op | source)
XLA Modules:
  0.0 61.6 jit_solution(6318412080037071683)
XLA Ops:
  1.3 56.8 %shard_map.110 = (bf16[2048,1024]{1,0:T(8,128)(2,1)S(1)}, bf16[2048,1024]{1,0:T(8,128)(2,1)S(1)}, f32[1,1024]{1,0:T(1,128)S(1)}, f32[1,1024]{1,0:T(1,128)S(1)}, bf16[64,2048]{1,0:T(8,128)(2,1)S(1)}) custom-call(f32[1,512,1024]{2,1,0:T(8,128)} %w_gate.1, f32[1,512,1024]{2,1,0:T(8,128)} %avg_gate.1, f32[1,512,1024]{2,1,0:T(8,128)} %w_up.1, ...), custom_call_target="tpu_custom_call" | custom-call | tf_op jit(solution)/shard_map/pallas_call | solution.py:257
  58.1 3.4 %shard_map.111 = (bf16[2048,1024]{1,0:T(8,128)(2,1)}, bf16[2048,1024]{1,0:T(8,128)(2,1)}, f32[1,1024]{1,0:T(1,128)}, f32[1,1024]{1,0:T(1,128)}, bf16[64,2048]{1,0:T(8,128)(2,1)}) custom-call(bf16[2048,1024]{1,0:T(8,128)(2,1)S(1)} %get-tuple-element.15.refs_0_, bf16[2048,1024]{1,0:T(8,128)(2,1)S(1)} %get-tuple-element.16.refs_1_, ...), custom_call_target="tpu_custom_call" | custom-call | tf_op jit(solution)/shard_map/pallas_call | solution.py:290

commit v4 on v3

v4 whole, which is shorter than its diff:
```python
import jax
import jax.numpy as jnp
from jax import lax
from jax.experimental import pallas as pl
from jax.experimental.pallas import tpu as pltpu
from jax.sharding import PartitionSpec as P

MESH = pl.DeviceIdType.MESH
LANES = 128
BLOCK = 64


PIECES = ((0, 0, 1), (0, 1, 2), (0, 3, 5), (1, 0, 4), (1, 4, 3), (1, 7, 1))
GROUPS = ((0,), (1,), (2,), (3, 4, 5))
TWICE = 128


def mix_and_send(
    w_gate, avg_gate, w_up, avg_up, mix_share, router_weight, router_gain,
    out_gate, out_up, out_scale_gate, out_scale_up, out_router,
    fresh, other, sums, router, share, factors,
    small_sem, load_sem, sum_send, sum_recv, across_send, across_recv, beside_send, beside_recv, passed_send, passed_recv,
    twice_send, twice_recv, router_send, router_recv, entered,
):
    rows, columns = fresh.shape[1], fresh.shape[2]
    pieces = len(PIECES)
    last = pieces - 1
    expert, shard = lax.axis_index("expert"), lax.axis_index("shard")
    far, core = shard // 2, shard % 2
    hi, y, x = expert // 16, (expert // 4) % 4, expert % 4
    across, beside, diagonal = (shard + 2) % 4, far * 2 + (1 - core), (1 - far) * 2 + (1 - core)
    peers = [(shard + d) % 4 for d in (1, 2, 3)]
    along_z = [(expert + 16 * d) % 64 for d in (1, 2, 3)]
    along_x = [hi * 16 + y * 4 + (x + d) % 4 for d in (1, 2, 3)]
    along_y = [hi * 16 + ((y + d) % 4) * 4 + x for d in (1, 2, 3)]

    def place(p):
        m, first, width = PIECES[p]
        return m, pl.ds(first * LANES, width * LANES)

    def load(p, which):
        m, cols = place(p)
        source = ((w_gate, avg_gate), (w_up, avg_up))[m][which]
        target = (fresh, other)[which]
        return pltpu.make_async_copy(source.at[0, :, cols], target.at[m, :, cols], load_sem.at[p, which])

    small = [
        pltpu.make_async_copy(mix_share, share, small_sem.at[0]),
        pltpu.make_async_copy(router_weight, factors.at[0], small_sem.at[1]),
        pltpu.make_async_copy(router_gain, factors.at[1], small_sem.at[2]),
    ]
    load(0, 0).start()
    load(0, 1).start()
    small[0].start()

    barrier = pltpu.get_barrier_semaphore()
    for p in peers:
        pl.semaphore_signal(barrier, inc=1, device_id=(expert, p), device_id_type=MESH)
    for p in range(1, pieces):
        load(p, 0).start()
        load(p, 1).start()
    router_peers = [(e, e > expert) for e in along_z + along_x + along_y]
    later = sum(after.astype(jnp.int32) for _, after in router_peers)
    for e, after in router_peers:

        @pl.when(after)
        def _():
            pl.semaphore_signal(barrier, inc=1, device_id=(e, shard), device_id_type=MESH)

    for copy in small[1:]:
        copy.start()
    small[0].wait()
    keep = share[0]
    rest = 1.0 - keep
    own = pl.multiple_of(shard * rows, rows)

    def blocks(p):
        m, first, width = PIECES[p]
        return m, [pl.ds((first + n) * LANES, LANES) for n in range(width)]

    def mix(p):
        load(p, 0).wait()
        load(p, 1).wait()
        m, parts = blocks(p)
        for cols in parts:

            def block(i, total):
                at = pl.ds(pl.multiple_of(i * BLOCK, BLOCK), BLOCK)
                value = keep * fresh[m, at, cols] + rest * other[m, at, cols]
                fresh[m, at, cols] = value
                return total + jnp.sum((value * value).reshape(BLOCK // 8, 8, LANES), axis=0)

            total = lax.fori_loop(0, rows // BLOCK, block, jnp.zeros((8, LANES), jnp.float32))
            sums[shard, :, pl.ds(m * columns + cols.start, LANES)] = jnp.sum(total, axis=0, keepdims=True)

    def sum_copies(g):
        m, first, _ = PIECES[GROUPS[g][0]]
        width = sum(PIECES[p][2] for p in GROUPS[g])
        part = sums.at[shard, :, pl.ds(m * columns + first * LANES, width * LANES)]
        return [
            pltpu.make_async_remote_copy(
                part, part, sum_send.at[g, d], sum_recv.at[g, d], device_id=(expert, peers[d]), device_id_type=MESH
            )
            for d in range(3)
        ]

    def mix_group(g):
        for p in GROUPS[g]:
            mix(p)

    def send_sums(g):
        for copy in sum_copies(g):
            copy.start()

    def wait_sums(g):
        for copy in sum_copies(g):
            copy.wait_recv()

    def moved(p, owner, start, count, device, send, recv):
        m, cols = place(p)
        piece = (out_gate, out_up)[m].at[pl.ds(pl.multiple_of(owner * rows + start, 128), count), cols]
        return pltpu.make_async_remote_copy(
            piece, piece, send, recv, device_id=(expert, device), device_id_type=MESH
        )

    def once(p):
        return rows - TWICE if p == last else rows

    def across_copy(p):
        return moved(p, shard, 0, once(p), across, across_send.at[p], across_recv.at[p])

    def beside_copy(p):
        return moved(p, shard, 0, rows, beside, beside_send.at[p], beside_recv.at[p])

    def passed_copy(p):
        return moved(p, across, 0, once(p), beside, passed_send.at[p], passed_recv.at[p])

    def twice_copies():
        return [
            moved(last, shard, rows - TWICE, TWICE, device, twice_send.at[n], twice_recv.at[n])
            for n, device in enumerate((across, diagonal))
        ]

    def scale_and_send(p):
        m, parts = blocks(p)
        target = (out_gate, out_up)[m]
        for cols in parts:
            at = pl.ds(m * columns + cols.start, LANES)
            scale = jnp.sqrt(sums[0, :, at] + sums[1, :, at] + sums[2, :, at] + sums[3, :, at])
            (out_scale_gate, out_scale_up)[m][:, cols] = scale
            inverse = 1.0 / scale

            def block(i, carry):
                at = pl.multiple_of(i * BLOCK, BLOCK)
                value = fresh[m, pl.ds(at, BLOCK), cols] * inverse
                target[pl.ds(pl.multiple_of(own + at, BLOCK), BLOCK), cols] = value.astype(jnp.bfloat16)
                return carry

            lax.fori_loop(0, rows // BLOCK, block, 0)
        across_copy(p).start()
        if p == last:
            for copy in twice_copies():
                copy.start()
        beside_copy(p).start()

    def pass_on(p):
        across_copy(p).wait_recv()
        passed_copy(p).start()

    def router_copy(piece, n, device):
        return pltpu.make_async_remote_copy(
            piece, piece, router_send.at[n], router_recv.at[n], device_id=device, device_id_type=MESH
        )

    tile = pl.multiple_of((expert % 16) * 8, 8)
    part = router.at[core, hi, pl.ds(pl.multiple_of(tile + far * 4, 4), 4)]
    mine = router.at[core, hi, pl.ds(tile, 8)]
    line = router.at[core, :, pl.ds(tile, 8)]
    plane = router.at[core, :, pl.ds(pl.multiple_of(y * 32, 32), 32)]
    stages = [
        [router_copy(part, 0, (expert, across))],
        [router_copy(mine, 1 + d, (along_z[d], shard)) for d in range(3)],
        [router_copy(line, 4 + d, (along_x[d], shard)) for d in range(3)],
        [router_copy(plane, 7 + d, (along_y[d], shard)) for d in range(3)],
        [router_copy(router.at[core], 10, (expert, beside))],
    ]

    def router_stage(n):
        if n > 0:
            for c in stages[n - 1]:
                c.wait_recv()
        if n < len(stages):
            for c in stages[n]:
                c.start()

    def put_router():
        for c in (0, 1):
            for f in (0, 1):
                for j in range(4):
                    at = (f * 2 + c) * 4 * LANES + j * LANES
                    for h in range(4):
                        piece = router[c, h, pl.ds(f * 4 + j, 16, stride=8), :]
                        out_router[h * 16 : (h + 1) * 16, at : at + LANES] = piece.astype(jnp.bfloat16)

    mix_group(0)
    pl.semaphore_wait(barrier, len(peers) + len(router_peers) - later)
    send_sums(0)
    for e, after in router_peers:

        @pl.when(jnp.logical_not(after))
        def _():
            pl.semaphore_signal(entered, inc=1, device_id=(e, shard), device_id_type=MESH)

    small[1].wait()
    small[2].wait()
    product = (factors[0] * factors[1]).astype(jnp.bfloat16).astype(jnp.float32)
    for j in range(4):
        router[core, hi, pl.ds(tile + far * 4 + j, 1)] = product[:, j * LANES : (j + 1) * LANES]
    mix_group(1)
    send_sums(1)
    router_stage(0)
    wait_sums(0)
    scale_and_send(0)
    mix_group(2)
    send_sums(2)
    wait_sums(1)
    scale_and_send(1)

    @pl.when(later > 0)
    def _():
        pl.semaphore_wait(entered, later)

    router_stage(1)
    mix_group(3)
    send_sums(3)
    wait_sums(2)
    scale_and_send(2)
    pass_on(0)
    wait_sums(3)
    scale_and_send(3)
    pass_on(1)
    router_stage(2)
    scale_and_send(4)
    scale_and_send(5)
    router_stage(3)
    router_stage(4)
    router_stage(5)
    put_router()
    pass_on(2)
    for g in range(len(GROUPS)):
        for copy in sum_copies(g):
            copy.wait_send()
    for stage in stages:
        for copy in stage:
            copy.wait_send()
    pass_on(3)
    for p in range(3):
        across_copy(p).wait_send()
        beside_copy(p).wait_send()
        beside_copy(p).wait_recv()
        passed_copy(p).wait_send()
        passed_copy(p).wait_recv()
    pass_on(4)
    for p in range(3, pieces):
        beside_copy(p).wait_send()
        beside_copy(p).wait_recv()
    pass_on(5)
    for p in range(3, pieces):
        across_copy(p).wait_send()
        passed_copy(p).wait_send()
        passed_copy(p).wait_recv()
    for copy in twice_copies():
        copy.wait_send()
        copy.wait_recv()


def put_out(*refs):
    sems = refs[10]
    copies = [pltpu.make_async_copy(refs[n], refs[n + 5], sems.at[n]) for n in range(5)]
    for copy in copies:
        copy.start()
    for copy in copies:
        copy.wait()


def per_device(w_gate, avg_gate, w_up, avg_up, mix_share, router_weight, router_gain):
    _, rows, columns = w_gate.shape
    pieces = len(PIECES)
    outs = pl.pallas_call(
        mix_and_send,
        out_shape=(
            pltpu.VMEM((4 * rows, columns), jnp.bfloat16),
            pltpu.VMEM((4 * rows, columns), jnp.bfloat16),
            pltpu.VMEM((1, columns), jnp.float32),
            pltpu.VMEM((1, columns), jnp.float32),
            pltpu.VMEM((64, 4 * rows), jnp.bfloat16),
        ),
        in_specs=[pl.BlockSpec(memory_space=pl.ANY)] * 7,
        out_specs=[pl.BlockSpec(memory_space=pltpu.VMEM)] * 5,
        scratch_shapes=[
            pltpu.VMEM((2, rows, columns), jnp.float32),
            pltpu.VMEM((2, rows, columns), jnp.float32),
            pltpu.VMEM((4, 1, 2 * columns), jnp.float32),
            pltpu.VMEM((2, 4, 128, LANES), jnp.float32),
            pltpu.SMEM((1,), jnp.float32),
            pltpu.VMEM((2, 1, rows), jnp.float32),
            pltpu.SemaphoreType.DMA((3,)),
            pltpu.SemaphoreType.DMA((pieces, 2)),
            pltpu.SemaphoreType.DMA((4, 3)),
            pltpu.SemaphoreType.DMA((4, 3)),
        ]
        + [pltpu.SemaphoreType.DMA((pieces,))] * 6
        + [pltpu.SemaphoreType.DMA((2,))] * 2
        + [pltpu.SemaphoreType.DMA((11,))] * 2
        + [pltpu.SemaphoreType.REGULAR],
        compiler_params=pltpu.CompilerParams(
            collective_id=0, has_side_effects=True, vmem_limit_bytes=55 * 1024 * 1024
        ),
    )(
        w_gate, avg_gate, w_up, avg_up, mix_share,
        router_weight.reshape(1, rows), router_gain.reshape(1, rows),
    )
    gate, up, scale_gate, scale_up, router = pl.pallas_call(
        put_out,
        out_shape=[jax.ShapeDtypeStruct(o.shape, o.dtype) for o in outs],
        in_specs=[pl.BlockSpec(memory_space=pltpu.VMEM)] * 5,
        out_specs=[pl.BlockSpec(memory_space=pl.ANY)] * 5,
        scratch_shapes=[pltpu.SemaphoreType.DMA((5,))],
        compiler_params=pltpu.CompilerParams(vmem_limit_bytes=1024 * 1024),
    )(*outs)
    return gate[None], up[None], scale_gate, scale_up, router.T


def solution(mesh):
    return jax.shard_map(
        per_device,
        mesh=mesh,
        in_specs=(
            P("expert", "shard", None),
            P("expert", "shard", None),
            P("expert", "shard", None),
            P("expert", "shard", None),
            P("expert"),
            P("shard", "expert"),
            P("shard"),
        ),
        out_specs=(
            P("expert", None, None),
            P("expert", None, None),
            P("expert", None),
            P("expert", None),
            P(),
        ),
        check_vma=False,
    )
```

time: 61.7 us -> 60.6 us (0.982)
  Pallas kernels: 60.3 us -> 59.3 us
    pallas_call x1, Pallas kernels: 56.8 us -> 55.8 us  [per_device(): pl.pallas_call(mix_and_send, out_shape=(pltpu.VMEM((4 * rows, columns), j...]
where the time goes in v4:
time: 60.6 us; the launch traced here: 60.5 us
  Pallas kernels  59.3 us (98%)
  between operations  1.29 us (2%)
    pallas_call x1, Pallas kernels, per_device(): pl.pallas_call(mix_and_send, out_shape=(pltpu.VMEM((4 * rows, columns), j...  55.8 us
    pallas_call x1, Pallas kernels, per_device(): pl.pallas_call(put_out, out_shape=[jax.ShapeDtypeStruct(o.shape, o.dtype)...  3.45 us

profile of v4, /device:TPU:1, one launch (start us, length us, event | category | flops | bytes accessed | tf_op | source)
XLA Modules:
  0.0 60.5 jit_solution(3390564400775101311)
XLA Ops:
  1.3 55.8 %shard_map.110 = (bf16[2048,1024]{1,0:T(8,128)(2,1)S(1)}, bf16[2048,1024]{1,0:T(8,128)(2,1)S(1)}, f32[1,1024]{1,0:T(1,128)S(1)}, f32[1,1024]{1,0:T(1,128)S(1)}, bf16[64,2048]{1,0:T(8,128)(2,1)S(1)}) custom-call(f32[1,512,1024]{2,1,0:T(8,128)} %w_gate.1, f32[1,512,1024]{2,1,0:T(8,128)} %avg_gate.1, f32[1,512,1024]{2,1,0:T(8,128)} %w_up.1, ...), custom_call_target="tpu_custom_call" | custom-call | tf_op jit(solution)/shard_map/pallas_call | solution.py:289
  57.1 3.4 %shard_map.111 = (bf16[2048,1024]{1,0:T(8,128)(2,1)}, bf16[2048,1024]{1,0:T(8,128)(2,1)}, f32[1,1024]{1,0:T(1,128)}, f32[1,1024]{1,0:T(1,128)}, bf16[64,2048]{1,0:T(8,128)(2,1)}) custom-call(bf16[2048,1024]{1,0:T(8,128)(2,1)S(1)} %get-tuple-element.15.refs_0_, bf16[2048,1024]{1,0:T(8,128)(2,1)S(1)} %get-tuple-element.16.refs_1_, ...), custom_call_target="tpu_custom_call" | custom-call | tf_op jit(solution)/shard_map/pallas_call | solution.py:323

commit v5 on v4

--- a/solution.py
+++ b/solution.py
@@ -10,17 +10,18 @@
 BLOCK = 64
 
 
-PIECES = ((0, 0, 1), (0, 1, 2), (0, 3, 5), (1, 0, 4), (1, 4, 3), (1, 7, 1))
-GROUPS = ((0,), (1,), (2,), (3, 4, 5))
+PIECES = ((0, 0, 1), (0, 1, 2), (0, 3, 5), (1, 0, 7), (1, 7, 1))
+GROUPS = ((0,), (1,), (2,), (3, 4))
 TWICE = 128
+RAW = 128
 
 
 def mix_and_send(
     w_gate, avg_gate, w_up, avg_up, mix_share, router_weight, router_gain,
     out_gate, out_up, out_scale_gate, out_scale_up, out_router,
-    fresh, other, sums, router, share, factors,
+    fresh, other, sums, router, share, factors, arrived,
     small_sem, load_sem, sum_send, sum_recv, across_send, across_recv, beside_send, beside_recv, passed_send, passed_recv,
-    twice_send, twice_recv, router_send, router_recv, entered,
+    twice_send, twice_recv, raw_send, raw_recv, router_send, router_recv, entered,
 ):
     rows, columns = fresh.shape[1], fresh.shape[2]
     pieces = len(PIECES)
@@ -49,13 +50,12 @@
         pltpu.make_async_copy(router_weight, factors.at[0], small_sem.at[1]),
         pltpu.make_async_copy(router_gain, factors.at[1], small_sem.at[2]),
     ]
+    barrier = pltpu.get_barrier_semaphore()
+    for p in peers:
+        pl.semaphore_signal(barrier, inc=1, device_id=(expert, p), device_id_type=MESH)
     load(0, 0).start()
     load(0, 1).start()
     small[0].start()
-
-    barrier = pltpu.get_barrier_semaphore()
-    for p in peers:
-        pl.semaphore_signal(barrier, inc=1, device_id=(expert, p), device_id_type=MESH)
     for p in range(1, pieces):
         load(p, 0).start()
         load(p, 1).start()
@@ -90,7 +90,7 @@
                 fresh[m, at, cols] = value
                 return total + jnp.sum((value * value).reshape(BLOCK // 8, 8, LANES), axis=0)
 
-            total = lax.fori_loop(0, rows // BLOCK, block, jnp.zeros((8, LANES), jnp.float32))
+            total = lax.fori_loop(0, rows // BLOCK, block, jnp.zeros((8, LANES), jnp.float32), unroll=True)
             sums[shard, :, pl.ds(m * columns + cols.start, LANES)] = jnp.sum(total, axis=0, keepdims=True)
 
     def sum_copies(g):
@@ -123,17 +123,15 @@
             piece, piece, send, recv, device_id=(expert, device), device_id_type=MESH
         )
 
-    def once(p):
-        return rows - TWICE if p == last else rows
-
     def across_copy(p):
-        return moved(p, shard, 0, once(p), across, across_send.at[p], across_recv.at[p])
+        start, stop = RAW if p == 0 else 0, rows - TWICE if p == last else rows
+        return moved(p, shard, start, stop - start, across, across_send.at[p], across_recv.at[p])
 
     def beside_copy(p):
         return moved(p, shard, 0, rows, beside, beside_send.at[p], beside_recv.at[p])
 
     def passed_copy(p):
-        return moved(p, across, 0, once(p), beside, passed_send.at[p], passed_recv.at[p])
+        return moved(p, across, 0, rows - TWICE if p == last else rows, beside, passed_send.at[p], passed_recv.at[p])
 
     def twice_copies():
         return [
@@ -141,12 +139,27 @@
             for n, device in enumerate((across, diagonal))
         ]
 
+    def raw_copy():
+        return pltpu.make_async_remote_copy(
+            fresh.at[0, pl.ds(0, RAW), pl.ds(0, LANES)], arrived, raw_send, raw_recv,
+            device_id=(expert, across), device_id_type=MESH,
+        )
+
+    def scale_of(m, cols):
+        at = pl.ds(m * columns + cols.start, LANES)
+        return jnp.sqrt(sums[0, :, at] + sums[1, :, at] + sums[2, :, at] + sums[3, :, at])
+
+    def scale_arrived():
+        cols = pl.ds(0, LANES)
+        raw_copy().wait_recv()
+        value = arrived[...] * (1.0 / scale_of(0, cols))
+        out_gate[pl.ds(pl.multiple_of(across * rows, rows), RAW), cols] = value.astype(jnp.bfloat16)
+
     def scale_and_send(p):
         m, parts = blocks(p)
         target = (out_gate, out_up)[m]
         for cols in parts:
-            at = pl.ds(m * columns + cols.start, LANES)
-            scale = jnp.sqrt(sums[0, :, at] + sums[1, :, at] + sums[2, :, at] + sums[3, :, at])
+            scale = scale_of(m, cols)
             (out_scale_gate, out_scale_up)[m][:, cols] = scale
             inverse = 1.0 / scale
 
@@ -156,7 +169,7 @@
                 target[pl.ds(pl.multiple_of(own + at, BLOCK), BLOCK), cols] = value.astype(jnp.bfloat16)
                 return carry
 
-            lax.fori_loop(0, rows // BLOCK, block, 0)
+            lax.fori_loop(0, rows // BLOCK, block, 0, unroll=True)
         across_copy(p).start()
         if p == last:
             for copy in twice_copies():
@@ -205,6 +218,7 @@
     mix_group(0)
     pl.semaphore_wait(barrier, len(peers) + len(router_peers) - later)
     send_sums(0)
+    raw_copy().start()
     for e, after in router_peers:
 
         @pl.when(jnp.logical_not(after))
@@ -219,10 +233,10 @@
     mix_group(1)
     send_sums(1)
     router_stage(0)
+    mix_group(2)
+    send_sums(2)
     wait_sums(0)
     scale_and_send(0)
-    mix_group(2)
-    send_sums(2)
     wait_sums(1)
     scale_and_send(1)
 
@@ -235,13 +249,13 @@
     send_sums(3)
     wait_sums(2)
     scale_and_send(2)
+    scale_arrived()
     pass_on(0)
     wait_sums(3)
     scale_and_send(3)
     pass_on(1)
     router_stage(2)
     scale_and_send(4)
-    scale_and_send(5)
     router_stage(3)
     router_stage(4)
     router_stage(5)
@@ -260,15 +274,15 @@
         beside_copy(p).wait_recv()
         passed_copy(p).wait_send()
         passed_copy(p).wait_recv()
-    pass_on(4)
     for p in range(3, pieces):
         beside_copy(p).wait_send()
         beside_copy(p).wait_recv()
-    pass_on(5)
+    pass_on(4)
     for p in range(3, pieces):
         across_copy(p).wait_send()
         passed_copy(p).wait_send()
         passed_copy(p).wait_recv()
+    raw_copy().wait_send()
     for copy in twice_copies():
         copy.wait_send()
         copy.wait_recv()
@@ -304,6 +318,7 @@
             pltpu.VMEM((2, 4, 128, LANES), jnp.float32),
             pltpu.SMEM((1,), jnp.float32),
             pltpu.VMEM((2, 1, rows), jnp.float32),
+            pltpu.VMEM((RAW, LANES), jnp.float32),
             pltpu.SemaphoreType.DMA((3,)),
             pltpu.SemaphoreType.DMA((pieces, 2)),
             pltpu.SemaphoreType.DMA((4, 3)),
@@ -311,6 +326,7 @@
         ]
         + [pltpu.SemaphoreType.DMA((pieces,))] * 6
         + [pltpu.SemaphoreType.DMA((2,))] * 2
+        + [pltpu.SemaphoreType.DMA(())] * 2
         + [pltpu.SemaphoreType.DMA((11,))] * 2
         + [pltpu.SemaphoreType.REGULAR],
         compiler_params=pltpu.CompilerParams(

time: 60.6 us -> 60.5 us (level)
  no operation moved by 1% of the time
where the time goes in v5:
time: 60.5 us; the launch traced here: 60.4 us
  Pallas kernels  59.1 us (98%)
  between operations  1.29 us (2%)
    pallas_call x1, Pallas kernels, per_device(): pl.pallas_call(mix_and_send, out_shape=(pltpu.VMEM((4 * rows, columns), j...  55.6 us
    pallas_call x1, Pallas kernels, per_device(): pl.pallas_call(put_out, out_shape=[jax.ShapeDtypeStruct(o.shape, o.dtype)...  3.45 us

profile of v5, /device:TPU:1, one launch (start us, length us, event | category | flops | bytes accessed | tf_op | source)
XLA Modules:
  0.0 60.4 jit_solution(436612568642872399)
XLA Ops:
  1.3 55.6 %shard_map.110 = (bf16[2048,1024]{1,0:T(8,128)(2,1)S(1)}, bf16[2048,1024]{1,0:T(8,128)(2,1)S(1)}, f32[1,1024]{1,0:T(1,128)S(1)}, f32[1,1024]{1,0:T(1,128)S(1)}, bf16[64,2048]{1,0:T(8,128)(2,1)S(1)}) custom-call(f32[1,512,1024]{2,1,0:T(8,128)} %w_gate.1, f32[1,512,1024]{2,1,0:T(8,128)} %avg_gate.1, f32[1,512,1024]{2,1,0:T(8,128)} %w_up.1, ...), custom_call_target="tpu_custom_call" | custom-call | tf_op jit(solution)/shard_map/pallas_call | solution.py:303
  56.9 3.4 %shard_map.111 = (bf16[2048,1024]{1,0:T(8,128)(2,1)}, bf16[2048,1024]{1,0:T(8,128)(2,1)}, f32[1,1024]{1,0:T(1,128)}, f32[1,1024]{1,0:T(1,128)}, bf16[64,2048]{1,0:T(8,128)(2,1)}) custom-call(bf16[2048,1024]{1,0:T(8,128)(2,1)S(1)} %get-tuple-element.15.refs_0_, bf16[2048,1024]{1,0:T(8,128)(2,1)S(1)} %get-tuple-element.16.refs_1_, ...), custom_call_target="tpu_custom_call" | custom-call | tf_op jit(solution)/shard_map/pallas_call | solution.py:339

commit v6 on v4

--- a/solution.py
+++ b/solution.py
@@ -10,8 +10,8 @@
 BLOCK = 64
 
 
-PIECES = ((0, 0, 1), (0, 1, 2), (0, 3, 5), (1, 0, 4), (1, 4, 3), (1, 7, 1))
-GROUPS = ((0,), (1,), (2,), (3, 4, 5))
+PIECES = ((0, 0, 1), (0, 1, 2), (0, 3, 5), (1, 0, 7), (1, 7, 1))
+GROUPS = ((0,), (1,), (2,), (3, 4))
 TWICE = 128
 
 
@@ -49,13 +49,12 @@
         pltpu.make_async_copy(router_weight, factors.at[0], small_sem.at[1]),
         pltpu.make_async_copy(router_gain, factors.at[1], small_sem.at[2]),
     ]
+    barrier = pltpu.get_barrier_semaphore()
+    for p in peers:
+        pl.semaphore_signal(barrier, inc=1, device_id=(expert, p), device_id_type=MESH)
     load(0, 0).start()
     load(0, 1).start()
     small[0].start()
-
-    barrier = pltpu.get_barrier_semaphore()
-    for p in peers:
-        pl.semaphore_signal(barrier, inc=1, device_id=(expert, p), device_id_type=MESH)
     for p in range(1, pieces):
         load(p, 0).start()
         load(p, 1).start()
@@ -90,7 +89,7 @@
                 fresh[m, at, cols] = value
                 return total + jnp.sum((value * value).reshape(BLOCK // 8, 8, LANES), axis=0)
 
-            total = lax.fori_loop(0, rows // BLOCK, block, jnp.zeros((8, LANES), jnp.float32))
+            total = lax.fori_loop(0, rows // BLOCK, block, jnp.zeros((8, LANES), jnp.float32), unroll=True)
             sums[shard, :, pl.ds(m * columns + cols.start, LANES)] = jnp.sum(total, axis=0, keepdims=True)
 
     def sum_copies(g):
@@ -156,7 +155,7 @@
                 target[pl.ds(pl.multiple_of(own + at, BLOCK), BLOCK), cols] = value.astype(jnp.bfloat16)
                 return carry
 
-            lax.fori_loop(0, rows // BLOCK, block, 0)
+            lax.fori_loop(0, rows // BLOCK, block, 0, unroll=True)
         across_copy(p).start()
         if p == last:
             for copy in twice_copies():
@@ -219,10 +218,10 @@
     mix_group(1)
     send_sums(1)
     router_stage(0)
+    mix_group(2)
+    send_sums(2)
     wait_sums(0)
     scale_and_send(0)
-    mix_group(2)
-    send_sums(2)
     wait_sums(1)
     scale_and_send(1)
 
@@ -241,7 +240,6 @@
     pass_on(1)
     router_stage(2)
     scale_and_send(4)
-    scale_and_send(5)
     router_stage(3)
     router_stage(4)
     router_stage(5)
@@ -260,11 +258,10 @@
         beside_copy(p).wait_recv()
         passed_copy(p).wait_send()
         passed_copy(p).wait_recv()
-    pass_on(4)
     for p in range(3, pieces):
         beside_copy(p).wait_send()
         beside_copy(p).wait_recv()
-    pass_on(5)
+    pass_on(4)
     for p in range(3, pieces):
         across_copy(p).wait_send()
         passed_copy(p).wait_send()

time: 60.6 us -> 60.4 us (level)
  no operation moved by 1% of the time
where the time goes in v6:
time: 60.4 us
  Pallas kernels  59.1 us (98%)
  between operations  1.29 us (2%)
    pallas_call x1, Pallas kernels, per_device(): pl.pallas_call(mix_and_send, out_shape=(pltpu.VMEM((4 * rows, columns), j...  55.6 us
    pallas_call x1, Pallas kernels, per_device(): pl.pallas_call(put_out, out_shape=[jax.ShapeDtypeStruct(o.shape, o.dtype)...  3.45 us

profile of v6, /device:TPU:1, one launch (start us, length us, event | category | flops | bytes accessed | tf_op | source)
XLA Modules:
  0.0 60.4 jit_solution(11784486801589677166)
XLA Ops:
  1.3 55.6 %shard_map.110 = (bf16[2048,1024]{1,0:T(8,128)(2,1)S(1)}, bf16[2048,1024]{1,0:T(8,128)(2,1)S(1)}, f32[1,1024]{1,0:T(1,128)S(1)}, f32[1,1024]{1,0:T(1,128)S(1)}, bf16[64,2048]{1,0:T(8,128)(2,1)S(1)}) custom-call(f32[1,512,1024]{2,1,0:T(8,128)} %w_gate.1, f32[1,512,1024]{2,1,0:T(8,128)} %avg_gate.1, f32[1,512,1024]{2,1,0:T(8,128)} %w_up.1, ...), custom_call_target="tpu_custom_call" | custom-call | tf_op jit(solution)/shard_map/pallas_call | solution.py:286
  56.9 3.4 %shard_map.111 = (bf16[2048,1024]{1,0:T(8,128)(2,1)}, bf16[2048,1024]{1,0:T(8,128)(2,1)}, f32[1,1024]{1,0:T(1,128)}, f32[1,1024]{1,0:T(1,128)}, bf16[64,2048]{1,0:T(8,128)(2,1)}) custom-call(bf16[2048,1024]{1,0:T(8,128)(2,1)S(1)} %get-tuple-element.15.refs_0_, bf16[2048,1024]{1,0:T(8,128)(2,1)S(1)} %get-tuple-element.16.refs_1_, ...), custom_call_target="tpu_custom_call" | custom-call | tf_op jit(solution)/shard_map/pallas_call | solution.py:320
